TPU v7x, 32 devices: a whole 2x2x4 slice. The times are simulated.
32 devices in a mesh: blk: 32 (over z, y, x, core).
Axes of the slice: x: 2, y: 2, z: 4, core: 2. Of those that a mesh axis runs over, the one named last changes fastest.
Arguments:
- tensor_blocks: bfloat16 [352, 32, 32, 1024], P('blk')
- block_index: int32 [352, 4], P('blk'), may hold values from 0 to 8, as said below
- starts: float32 [256, 32], P(None, 'blk'), may hold values from -6 to 6
- shifts: float32 [32], replicated, may hold values from 0.5 to 2
Outputs:
- iterate: float32 [256, 32], P(None, 'blk')
- estimate: float32 [32], P('blk')
Inputs may be any that keep to these rules, and one draw needn't show every extreme that they name: `block_index`: every sorted quadruple i <= j <= k <= l of 0 to 7 is held by exactly one slot; every other slot holds 8 in all four entries and is not used. A live slot's block is unchanged when two of its axes with equal block indices are swapped.
All inputs are finite; a program needn't handle non-finite values.
Results may differ from a plain program's by a relative error of at most 0.009.
Values sent between devices are 32-bit elements; how exact they have to be, the bound alone decides.
No kernel may reach another device: no remote copies, remote signals or barrier semaphores. Data moves between devices by JAX's collectives and lax.ppermute only.
A program may use at most 192 MiB of HBM per device.

v0:
```python
import jax
import jax.numpy as jnp
from jax import lax
from jax.sharding import PartitionSpec as P

NSIZE = 256
ITERS = 2
letters = "abcd"


def normalize(values):
    return values * lax.rsqrt(jnp.mean(values * values, axis=0) + 1e-06)


def equal_counts(indices, position):
    earlier = jnp.float32(0.0)
    same_count = jnp.float32(0.0)
    for other in range(4):
        match_value = (indices[other] == indices[position]).astype(jnp.float32)
        same_count = same_count + match_value
        if other < position:
            earlier = earlier + match_value
    return (earlier, same_count)


def factor_product(indices):
    product = jnp.float32(1.0)
    for other in range(1, 4):
        earlier, unused = equal_counts(indices, other)
        product = product * (1.0 + earlier)
    return product


def contract_axis(tensor, pieces, position):
    others = [other for other in range(4) if other != position]
    leading = others[0]
    paired = (pieces[others[1]][:, None, :] * pieces[others[2]][None, :, :]).astype(jnp.bfloat16)
    kept = "".join(sorted(letters[position] + letters[leading]))
    pattern = "abcd," + letters[others[1]] + letters[others[2]] + "r->" + kept + "r"
    partial_sum = jnp.einsum(pattern, tensor, paired, preferred_element_type=jnp.float32)
    if position < leading:
        return jnp.sum(partial_sum * pieces[leading][None, :, :], axis=1)
    return jnp.sum(partial_sum * pieces[leading][:, None, :], axis=0)


def apply_tensor(tensor_blocks, block_index, current):
    tile_size = tensor_blocks.shape[1]
    blocks_count = NSIZE // tile_size
    total = jnp.zeros(current.shape, jnp.float32)
    for slot_id in range(tensor_blocks.shape[0]):
        tensor = tensor_blocks[slot_id].reshape(tile_size, tile_size, tile_size, tile_size)
        indices = block_index[slot_id]
        live = (indices[0] < blocks_count).astype(jnp.float32)
        safe = jnp.minimum(indices, blocks_count - 1)
        pieces = [
            lax.dynamic_slice_in_dim(current, safe[other] * tile_size, tile_size, 0)
            for other in range(4)
        ]
        weight = live * 6.0 / factor_product(indices)
        for position in range(4):
            result = weight * contract_axis(tensor, pieces, position)
            start = safe[position] * tile_size
            total = lax.dynamic_update_slice_in_dim(
                total, lax.dynamic_slice_in_dim(total, start, tile_size, 0) + result, start, 0
            )
    return total


def body(tensor_blocks, block_index, starts, shifts):
    own_count = starts.shape[1]
    offset = lax.axis_index("blk") * own_count
    own_shifts = lax.dynamic_slice_in_dim(shifts, offset, own_count, 0)
    current_own = normalize(starts)
    current = lax.all_gather(current_own, "blk", axis=1, tiled=True)
    previous_own = current_own
    image_own = current_own
    for step_id in range(ITERS):
        applied = apply_tensor(tensor_blocks, block_index, current)
        final_turn = step_id == ITERS - 1
        summed = lax.psum(applied, "blk")
        image_own = lax.dynamic_slice_in_dim(summed, offset, own_count, 1)
        previous_own = lax.dynamic_slice_in_dim(current, offset, own_count, 1)
        if final_turn:
            current_own = normalize(image_own + own_shifts[None, :] * previous_own)
        else:
            current = normalize(summed + shifts[None, :] * current)
    estimate = jnp.mean(previous_own * image_own, axis=0) * lax.rsqrt(
        jnp.mean(image_own * image_own, axis=0) + 1e-06
    )
    return (current_own, estimate)


def solution(mesh):
    placed = (P("blk", None, None, None), P("blk", None), P(None, "blk"), P())
    return jax.shard_map(
        body, mesh=mesh, in_specs=placed, out_specs=(P(None, "blk"), P("blk")), check_vma=False
    )
```

profile of v0, /device:TPU:0, one launch (start us, length us, event | category | flops | bytes accessed | tf_op | source)
XLA Modules:
  0.0 739.3 jit_solution(965814484213138154)
XLA Ops:
  5.7 43.3 %all-gather = f32[32,1,256]{2,1,0:T(1,128)S(1)} all-gather(f32[1,1,256]{2,1,0:T(1,128)S(1)} %multiply_bitcast_fusion), channel_id=1, replica_groups=mesh['blk'=32] {'blk'}, dimensions={0}, use_global_device_ids=true | all-gather | bytes 33792 | tf_op jit(solution)/shard_map/all_gather | solution.py:74
  63.7 15.7 %fusion.548 = (bf16[1,32,32,1024]{3,2,1,0:T(8,128)(2,1)S(1)}, bf16[1,32,32,1024]{3,2,1,0:T(8,128)(2,1)}, bf16[1,32,32,1024]{3,2,1,0:T(8,128)(2,1)}, bf16[1,32,32...) fusion(bf16[11,32,32,1024]{3,2,1,0:T(8,128)(2,1)} %param.4), kind=kLoop, calls=%fused_computation.877 | loop fusion | bytes 46137344 | tf_op jit(solution)/shard_map/slice | solution.py:51
  79.4 10.9 %reshape_squeeze.44 = bf16[32,32,32,32]{3,2,1,0:T(8,128)(2,1)} reshape(bf16[1,32,32,1024]{3,2,1,0:T(8,128)(2,1)} %get-tuple-element.60) | data formatting | bytes 4194304 | tf_op jit(solution)/shard_map/reshape;squeeze | solution.py:51
  95.9 6.1 multiply_reduce_fusion.42
  128.8 11.3 %reshape_squeeze.45 = bf16[32,32,32,32]{3,2,1,0:T(8,128)(2,1)} reshape(bf16[1,32,32,1024]{3,2,1,0:T(8,128)(2,1)} %get-tuple-element.59) | data formatting | bytes 4194304 | tf_op jit(solution)/shard_map/reshape;squeeze | solution.py:51
  140.2 6.1 multiply_reduce_fusion.40
  161.1 11.0 %reshape_squeeze.46 = bf16[32,32,32,32]{3,2,1,0:T(8,128)(2,1)} reshape(bf16[1,32,32,1024]{3,2,1,0:T(8,128)(2,1)} %get-tuple-element.58) | data formatting | bytes 4194304 | tf_op jit(solution)/shard_map/reshape;squeeze | solution.py:51
  172.2 6.1 multiply_reduce_fusion.38
  188.6 3.6 fusion.192
  192.3 11.1 %reshape_squeeze.47 = bf16[32,32,32,32]{3,2,1,0:T(8,128)(2,1)} reshape(bf16[1,32,32,1024]{3,2,1,0:T(8,128)(2,1)} %get-tuple-element.57) | data formatting | bytes 4194304 | tf_op jit(solution)/shard_map/reshape;squeeze | solution.py:51
  203.5 6.1 multiply_reduce_fusion.36
  220.0 3.6 fusion.190
  223.7 11.1 %reshape_squeeze.48 = bf16[32,32,32,32]{3,2,1,0:T(8,128)(2,1)} reshape(bf16[1,32,32,1024]{3,2,1,0:T(8,128)(2,1)} %get-tuple-element.56) | data formatting | bytes 4194304 | tf_op jit(solution)/shard_map/reshape;squeeze | solution.py:51
  234.9 6.1 multiply_reduce_fusion.34
  255.3 11.4 %reshape_squeeze.49 = bf16[32,32,32,32]{3,2,1,0:T(8,128)(2,1)} reshape(bf16[1,32,32,1024]{3,2,1,0:T(8,128)(2,1)} %get-tuple-element.55) | data formatting | bytes 4194304 | tf_op jit(solution)/shard_map/reshape;squeeze | solution.py:51
  266.8 6.1 multiply_reduce_fusion.32
  283.3 3.6 fusion.186
  287.1 11.0 %reshape_squeeze.50 = bf16[32,32,32,32]{3,2,1,0:T(8,128)(2,1)} reshape(bf16[1,32,32,1024]{3,2,1,0:T(8,128)(2,1)} %get-tuple-element.54) | data formatting | bytes 4194304 | tf_op jit(solution)/shard_map/reshape;squeeze | solution.py:51
  298.2 6.1 multiply_reduce_fusion.30
  319.5 11.1 %reshape_squeeze.51 = bf16[32,32,32,32]{3,2,1,0:T(8,128)(2,1)} reshape(bf16[1,32,32,1024]{3,2,1,0:T(8,128)(2,1)} %get-tuple-element.53) | data formatting | bytes 4194304 | tf_op jit(solution)/shard_map/reshape;squeeze | solution.py:51
  330.6 6.1 multiply_reduce_fusion.28
  347.2 3.6 fusion.182
  350.9 11.1 %reshape_squeeze.52 = bf16[32,32,32,32]{3,2,1,0:T(8,128)(2,1)} reshape(bf16[1,32,32,1024]{3,2,1,0:T(8,128)(2,1)} %get-tuple-element.52) | data formatting | bytes 4194304 | tf_op jit(solution)/shard_map/reshape;squeeze | solution.py:51
  362.1 6.1 multiply_reduce_fusion.26
  378.9 3.6 fusion.180
  382.7 11.3 %reshape_squeeze.53 = bf16[32,32,32,32]{3,2,1,0:T(8,128)(2,1)} reshape(bf16[1,32,32,1024]{3,2,1,0:T(8,128)(2,1)} %get-tuple-element.61) | data formatting | bytes 4194304 | tf_op jit(solution)/shard_map/reshape;squeeze | solution.py:51
  394.1 6.1 multiply_reduce_fusion.24
  414.6 8.1 %reshape_squeeze.54 = bf16[32,32,32,32]{3,2,1,0:T(8,128)(2,1)} reshape(bf16[1,32,32,1024]{3,2,1,0:T(8,128)(2,1)S(1)} %get-tuple-element.51) | data formatting | bytes 4194304 | tf_op jit(solution)/shard_map/reshape;squeeze | solution.py:51
  422.7 6.1 multiply_reduce_fusion.22
  443.2 38.1 %psum.14 = f32[256,32]{1,0:T(8,128)S(1)} all-reduce(f32[256,32]{1,0:T(8,128)S(1)} %constant_dynamic-update-slice_fusion.44), channel_id=1, replica_groups=mesh['blk'=32] {'blk'}, use_global_device_ids=true, to_apply=%region_45.0 | all-reduce | flops 8192 | bytes 65536 | tf_op jit(solution)/shard_map/psum | solution.py:80
  481.6 5.9 multiply_reduce_fusion.20
  487.6 5.8 fusion.175
  493.4 6.9 fusion.174
  500.4 5.9 multiply_reduce_fusion.18
  506.3 5.8 fusion.173
  512.2 7.3 fusion.172
  519.7 5.9 multiply_reduce_fusion.16
  525.6 5.8 fusion.171
  531.5 6.9 fusion.170
  538.5 6.1 multiply_reduce_fusion.14
  544.6 5.8 fusion.169
  550.5 6.9 fusion.168
  557.5 5.9 multiply_reduce_fusion.12
  563.4 5.8 fusion.167
  569.3 7.1 fusion.166
  576.5 5.9 multiply_reduce_fusion.10
  582.4 5.8 fusion.165
  588.3 6.9 fusion.164
  595.4 5.9 multiply_reduce_fusion.8
  601.3 6.2 fusion.163
  607.6 6.9 fusion.162
  614.6 5.9 multiply_reduce_fusion.6
  620.5 5.8 fusion.161
  626.4 6.9 fusion.160
  633.4 6.1 multiply_reduce_fusion.4
  639.5 5.8 fusion.159
  645.4 6.9 fusion.158
  652.4 5.9 multiply_reduce_fusion.2
  658.3 5.8 fusion.157
  664.2 7.1 fusion.156
  671.4 5.9 multiply_reduce_fusion
  677.3 5.8 fusion.155
  683.1 6.9 fusion.154
  690.1 42.2 %psum.15 = f32[256,32]{1,0:T(8,128)S(1)} all-reduce(f32[256,32]{1,0:T(8,128)S(1)} %constant_dynamic-update-slice_fusion), channel_id=1, replica_groups=mesh['blk'=32] {'blk'}, use_global_device_ids=true, to_apply=%region_91.0 | all-reduce | flops 8192 | bytes 65536 | tf_op jit(solution)/shard_map/psum | solution.py:80
  (214 shorter events, 67.3 us)
Async XLA Ops:
  90.3 11.7 %copy-start.11 = (s32[11,4]{0,1:T(4,128)S(1)}, s32[11,4]{0,1:T(4,128)}, u32[]{:S(2)}) copy-start(s32[11,4]{0,1:T(4,128)} %param.5) | copy-start | bytes 532
  95.9 14.8 %copy-start = (bf16[32,32,32,32]{3,2,1,0:T(8,128)(2,1)S(1)}, bf16[32,32,32,32]{3,2,1,0:T(8,128)(2,1)}, u32[]{:S(2)}) copy-start(bf16[32,32,32,32]{3,2,1,0:T(8,128)(2,1)} %reshape_squeeze.44) | copy-start | bytes 6291460
  140.2 14.7 %copy-start.1 = (bf16[32,32,32,32]{3,2,1,0:T(8,128)(2,1)S(1)}, bf16[32,32,32,32]{3,2,1,0:T(8,128)(2,1)}, u32[]{:S(2)}) copy-start(bf16[32,32,32,32]{3,2,1,0:T(8,128)(2,1)} %reshape_squeeze.45) | copy-start | bytes 6291460
  172.2 14.0 %copy-start.2 = (bf16[32,32,32,32]{3,2,1,0:T(8,128)(2,1)S(1)}, bf16[32,32,32,32]{3,2,1,0:T(8,128)(2,1)}, u32[]{:S(2)}) copy-start(bf16[32,32,32,32]{3,2,1,0:T(8,128)(2,1)} %reshape_squeeze.46) | copy-start | bytes 6291460
  203.5 14.1 %copy-start.3 = (bf16[32,32,32,32]{3,2,1,0:T(8,128)(2,1)S(1)}, bf16[32,32,32,32]{3,2,1,0:T(8,128)(2,1)}, u32[]{:S(2)}) copy-start(bf16[32,32,32,32]{3,2,1,0:T(8,128)(2,1)} %reshape_squeeze.47) | copy-start | bytes 6291460
  234.9 14.3 %copy-start.4 = (bf16[32,32,32,32]{3,2,1,0:T(8,128)(2,1)S(1)}, bf16[32,32,32,32]{3,2,1,0:T(8,128)(2,1)}, u32[]{:S(2)}) copy-start(bf16[32,32,32,32]{3,2,1,0:T(8,128)(2,1)} %reshape_squeeze.48) | copy-start | bytes 6291460
  266.8 14.2 %copy-start.5 = (bf16[32,32,32,32]{3,2,1,0:T(8,128)(2,1)S(1)}, bf16[32,32,32,32]{3,2,1,0:T(8,128)(2,1)}, u32[]{:S(2)}) copy-start(bf16[32,32,32,32]{3,2,1,0:T(8,128)(2,1)} %reshape_squeeze.49) | copy-start | bytes 6291460
  298.2 15.1 %copy-start.6 = (bf16[32,32,32,32]{3,2,1,0:T(8,128)(2,1)S(1)}, bf16[32,32,32,32]{3,2,1,0:T(8,128)(2,1)}, u32[]{:S(2)}) copy-start(bf16[32,32,32,32]{3,2,1,0:T(8,128)(2,1)} %reshape_squeeze.50) | copy-start | bytes 6291460
  330.6 14.1 %copy-start.7 = (bf16[32,32,32,32]{3,2,1,0:T(8,128)(2,1)S(1)}, bf16[32,32,32,32]{3,2,1,0:T(8,128)(2,1)}, u32[]{:S(2)}) copy-start(bf16[32,32,32,32]{3,2,1,0:T(8,128)(2,1)} %reshape_squeeze.51) | copy-start | bytes 6291460
  362.1 14.4 %copy-start.8 = (bf16[32,32,32,32]{3,2,1,0:T(8,128)(2,1)S(1)}, bf16[32,32,32,32]{3,2,1,0:T(8,128)(2,1)}, u32[]{:S(2)}) copy-start(bf16[32,32,32,32]{3,2,1,0:T(8,128)(2,1)} %reshape_squeeze.52) | copy-start | bytes 6291460
  394.1 14.4 %copy-start.9 = (bf16[32,32,32,32]{3,2,1,0:T(8,128)(2,1)S(1)}, bf16[32,32,32,32]{3,2,1,0:T(8,128)(2,1)}, u32[]{:S(2)}) copy-start(bf16[32,32,32,32]{3,2,1,0:T(8,128)(2,1)} %reshape_squeeze.53) | copy-start | bytes 6291460
  422.7 14.4 %copy-start.10 = (bf16[32,32,32,32]{3,2,1,0:T(8,128)(2,1)S(1)}, bf16[32,32,32,32]{3,2,1,0:T(8,128)(2,1)}, u32[]{:S(2)}) copy-start(bf16[32,32,32,32]{3,2,1,0:T(8,128)(2,1)} %reshape_squeeze.54) | copy-start | bytes 6291460
  437.2 44.2 %copy-start.12 = (f32[32]{0:T(128)S(1)}, f32[32]{0:T(128)}, u32[]{:S(2)}) copy-start(f32[32]{0:T(128)} %param.7) | copy-start | bytes 388
where the time goes:
time: 754 us; the launch traced here: 739 us
  matrix products  338 us (45%)
  local copies, waits for them, and re-layouts  148 us (20%)
  blocking collectives  124 us (16%)
  between operations  122 us (16%)
    dot_general x66, matrix products, contract_axis(): jnp.einsum(pattern, tensor, paired, preferred_element_type=jnp.float32)  338 us
    another operation x11, local copies, waits for them, and re-layouts, apply_tensor(): tensor_blocks[slot_id].reshape(tile_size, tile_size, tile_size, tile_size)  119 us
    psum x2, blocking collectives, body(): summed = lax.psum(applied, 'blk')  80.3 us
    all_gather x1, blocking collectives, body(): current = lax.all_gather(current_own, 'blk', axis=1, tiled=True)  43.3 us
    slice x1, local copies, waits for them, and re-layouts, apply_tensor(): tensor_blocks[slot_id].reshape(tile_size, tile_size, tile_size, tile_size)  15.7 us

commit v1 on v0

--- a/solution.py
+++ b/solution.py
@@ -77,7 +77,9 @@
     for step_id in range(ITERS):
         applied = apply_tensor(tensor_blocks, block_index, current)
         final_turn = step_id == ITERS - 1
-        summed = lax.psum(applied, "blk")
+        summed = applied
+        for hop in (1, 2, 4, 8, 16):
+            summed = summed + lax.ppermute(summed, "blk", [(dev, dev ^ hop) for dev in range(32)])
         image_own = lax.dynamic_slice_in_dim(summed, offset, own_count, 1)
         previous_own = lax.dynamic_slice_in_dim(current, offset, own_count, 1)
         if final_turn:

time: 754 us -> 694 us (0.920)
  blocking collectives: 124 us -> 43.3 us
  waiting for transfers between devices: 0 us -> 45.5 us
  matrix products: 338 us -> 312 us
    psum x2 -> x0, blocking collectives: 80.3 us -> none  [body(): summed = lax.psum(applied, 'blk')]
    ppermute x0 -> x10, waiting for transfers between devices: none -> 45.5 us  [body(): lax.ppermute(summed, 'blk', [(dev, dev ^ hop) for dev in range(32)])]
    dot_general x66, matrix products: 338 us -> 312 us  [contract_axis(): jnp.einsum(pattern, tensor, paired, preferred_element_type=jnp.float32)]
  transfers between devices with their start and end apart: 0 -> 10, of which waited for: 0 -> 10; matrix products, arithmetic and copies ran while one was open for 0% -> 0% of each run, Pallas kernels for 0% -> 0%
where the time goes in v1:
time: 694 us; the launch traced here: 685 us
  matrix products  312 us (45%)
  local copies, waits for them, and re-layouts  152 us (22%)
  between operations  124 us (18%)
  waiting for transfers between devices  45.5 us (7%)
  blocking collectives  43.3 us (6%)
    dot_general x66, matrix products, contract_axis(): jnp.einsum(pattern, tensor, paired, preferred_element_type=jnp.float32)  312 us
    another operation x11, local copies, waits for them, and re-layouts, apply_tensor(): tensor_blocks[slot_id].reshape(tile_size, tile_size, tile_size, tile_size)  119 us
    ppermute x10, waiting for transfers between devices, body(): lax.ppermute(summed, 'blk', [(dev, dev ^ hop) for dev in range(32)])  45.5 us
    all_gather x1, blocking collectives, body(): current = lax.all_gather(current_own, 'blk', axis=1, tiled=True)  43.3 us
    slice x1, local copies, waits for them, and re-layouts, apply_tensor(): tensor_blocks[slot_id].reshape(tile_size, tile_size, tile_size, tile_size)  16.3 us
  transfers between devices with their start and end apart: 10, of which 10 were waited for; matrix products, arithmetic and copies ran while one was open for 0% of the time, Pallas kernels for 0%

profile of v1, /device:TPU:0, one launch (start us, length us, event | category | flops | bytes accessed | tf_op | source)
XLA Modules:
  0.0 685.2 jit_solution(5925456788241654131)
XLA Ops:
  130.3 43.3 %all-gather = f32[32,1,256]{2,1,0:T(1,128)S(1)} all-gather(f32[1,1,256]{2,1,0:T(1,128)S(1)} %multiply_bitcast_fusion), channel_id=1, replica_groups=mesh['blk'=32] {'blk'}, dimensions={0}, use_global_device_ids=true | all-gather | bytes 33792 | tf_op jit(solution)/shard_map/all_gather | solution.py:74
  175.7 16.3 %fusion.548 = (bf16[1,32,32,1024]{3,2,1,0:T(8,128)(2,1)S(1)}, bf16[1,32,32,1024]{3,2,1,0:T(8,128)(2,1)}, bf16[1,32,32,1024]{3,2,1,0:T(8,128)(2,1)}, bf16[1,32,32...) fusion(bf16[11,32,32,1024]{3,2,1,0:T(8,128)(2,1)} %param.4), kind=kLoop, calls=%fused_computation.878 | loop fusion | bytes 46137344 | tf_op jit(solution)/shard_map/slice | solution.py:51
  192.0 10.9 %reshape_squeeze.45 = bf16[32,32,32,32]{3,2,1,0:T(8,128)(2,1)} reshape(bf16[1,32,32,1024]{3,2,1,0:T(8,128)(2,1)} %get-tuple-element.62) | data formatting | bytes 4194304 | tf_op jit(solution)/shard_map/reshape;squeeze | solution.py:51
  202.9 7.1 %fusion.194 = f32[32,32]{1,0:T(8,128)S(1)} fusion(bf16[32,32,32,32]{3,2,1,0:T(8,128)(2,1)} %reshape_squeeze.45, f32[32,32]{0,1:T(8,128)S(1)} %bitcast.1072, f32[32,32]{1,0:T(8,128)S(1)} %copy.361, f32[32,32]{1,0:T(8,128)S(1)} %copy.363), kind=kOutput, calls=%fused_computation.194 | convolution fusion | flops 67238912 | bytes 2113536 | tf_op jit(solution)/shard_map/abcd,bcr->adr/dot_general | solution.py:40
  215.0 11.0 %reshape_squeeze.44 = bf16[32,32,32,32]{3,2,1,0:T(8,128)(2,1)} reshape(bf16[1,32,32,1024]{3,2,1,0:T(8,128)(2,1)} %get-tuple-element.63) | data formatting | bytes 4194304 | tf_op jit(solution)/shard_map/reshape;squeeze | solution.py:51
  226.2 7.1 %fusion.196 = f32[32,32]{1,0:T(8,128)S(1)} fusion(bf16[32,32,32,32]{3,2,1,0:T(8,128)(2,1)} %reshape_squeeze.44, f32[32,32]{0,1:T(8,128)S(1)} %bitcast.1070, f32[32,32]{1,0:T(8,128)S(1)} %copy.351, f32[32,32]{1,0:T(8,128)S(1)} %copy.353), kind=kOutput, calls=%fused_computation.196 | convolution fusion | flops 67238912 | bytes 2113536 | tf_op jit(solution)/shard_map/abcd,bcr->adr/dot_general | solution.py:40
  238.4 11.1 %reshape_squeeze.46 = bf16[32,32,32,32]{3,2,1,0:T(8,128)(2,1)} reshape(bf16[1,32,32,1024]{3,2,1,0:T(8,128)(2,1)} %get-tuple-element.61) | data formatting | bytes 4194304 | tf_op jit(solution)/shard_map/reshape;squeeze | solution.py:51
  249.5 7.1 %fusion.192 = f32[32,32]{1,0:T(8,128)S(1)} fusion(bf16[32,32,32,32]{3,2,1,0:T(8,128)(2,1)} %reshape_squeeze.46, f32[32,32]{0,1:T(8,128)S(1)} %bitcast.1068, f32[32,32]{1,0:T(8,128)S(1)} %copy.371, f32[32,32]{1,0:T(8,128)S(1)} %copy.373), kind=kOutput, calls=%fused_computation.192 | convolution fusion | flops 67238912 | bytes 2113536 | tf_op jit(solution)/shard_map/abcd,bcr->adr/dot_general | solution.py:40
  261.8 11.1 %reshape_squeeze.47 = bf16[32,32,32,32]{3,2,1,0:T(8,128)(2,1)} reshape(bf16[1,32,32,1024]{3,2,1,0:T(8,128)(2,1)} %get-tuple-element.60) | data formatting | bytes 4194304 | tf_op jit(solution)/shard_map/reshape;squeeze | solution.py:51
  272.9 7.1 %fusion.190 = f32[32,32]{1,0:T(8,128)S(1)} fusion(bf16[32,32,32,32]{3,2,1,0:T(8,128)(2,1)} %reshape_squeeze.47, f32[32,32]{0,1:T(8,128)S(1)} %bitcast.1066, f32[32,32]{1,0:T(8,128)S(1)} %copy.381, f32[32,32]{1,0:T(8,128)S(1)} %copy.383), kind=kOutput, calls=%fused_computation.190 | convolution fusion | flops 67238912 | bytes 2113536 | tf_op jit(solution)/shard_map/abcd,bcr->adr/dot_general | solution.py:40
  285.1 11.3 %reshape_squeeze.48 = bf16[32,32,32,32]{3,2,1,0:T(8,128)(2,1)} reshape(bf16[1,32,32,1024]{3,2,1,0:T(8,128)(2,1)} %get-tuple-element.59) | data formatting | bytes 4194304 | tf_op jit(solution)/shard_map/reshape;squeeze | solution.py:51
  296.5 7.1 %fusion.188 = f32[32,32]{1,0:T(8,128)S(1)} fusion(bf16[32,32,32,32]{3,2,1,0:T(8,128)(2,1)} %reshape_squeeze.48, f32[32,32]{0,1:T(8,128)S(1)} %bitcast.1064, f32[32,32]{1,0:T(8,128)S(1)} %copy.391, f32[32,32]{1,0:T(8,128)S(1)} %copy.393), kind=kOutput, calls=%fused_computation.188 | convolution fusion | flops 67238912 | bytes 2113536 | tf_op jit(solution)/shard_map/abcd,bcr->adr/dot_general | solution.py:40
  308.7 11.1 %reshape_squeeze.49 = bf16[32,32,32,32]{3,2,1,0:T(8,128)(2,1)} reshape(bf16[1,32,32,1024]{3,2,1,0:T(8,128)(2,1)} %get-tuple-element.58) | data formatting | bytes 4194304 | tf_op jit(solution)/shard_map/reshape;squeeze | solution.py:51
  319.8 7.1 %fusion.186 = f32[32,32]{1,0:T(8,128)S(1)} fusion(bf16[32,32,32,32]{3,2,1,0:T(8,128)(2,1)} %reshape_squeeze.49, f32[32,32]{0,1:T(8,128)S(1)} %bitcast.1062, f32[32,32]{1,0:T(8,128)S(1)} %copy.401, f32[32,32]{1,0:T(8,128)S(1)} %copy.403), kind=kOutput, calls=%fused_computation.186 | convolution fusion | flops 67238912 | bytes 2113536 | tf_op jit(solution)/shard_map/abcd,bcr->adr/dot_general | solution.py:40
  332.0 11.1 %reshape_squeeze.50 = bf16[32,32,32,32]{3,2,1,0:T(8,128)(2,1)} reshape(bf16[1,32,32,1024]{3,2,1,0:T(8,128)(2,1)} %get-tuple-element.57) | data formatting | bytes 4194304 | tf_op jit(solution)/shard_map/reshape;squeeze | solution.py:51
  343.1 7.1 %fusion.184 = f32[32,32]{1,0:T(8,128)S(1)} fusion(bf16[32,32,32,32]{3,2,1,0:T(8,128)(2,1)} %reshape_squeeze.50, f32[32,32]{0,1:T(8,128)S(1)} %bitcast.1060, f32[32,32]{1,0:T(8,128)S(1)} %copy.411, f32[32,32]{1,0:T(8,128)S(1)} %copy.413), kind=kOutput, calls=%fused_computation.184 | convolution fusion | flops 67238912 | bytes 2113536 | tf_op jit(solution)/shard_map/abcd,bcr->adr/dot_general | solution.py:40
  355.3 11.1 %reshape_squeeze.51 = bf16[32,32,32,32]{3,2,1,0:T(8,128)(2,1)} reshape(bf16[1,32,32,1024]{3,2,1,0:T(8,128)(2,1)} %get-tuple-element.56) | data formatting | bytes 4194304 | tf_op jit(solution)/shard_map/reshape;squeeze | solution.py:51
  366.5 7.1 %fusion.182 = f32[32,32]{1,0:T(8,128)S(1)} fusion(bf16[32,32,32,32]{3,2,1,0:T(8,128)(2,1)} %reshape_squeeze.51, f32[32,32]{0,1:T(8,128)S(1)} %bitcast.1058, f32[32,32]{1,0:T(8,128)S(1)} %copy.421, f32[32,32]{1,0:T(8,128)S(1)} %copy.423), kind=kOutput, calls=%fused_computation.182 | convolution fusion | flops 67238912 | bytes 2113536 | tf_op jit(solution)/shard_map/abcd,bcr->adr/dot_general | solution.py:40
  378.7 11.3 %reshape_squeeze.52 = bf16[32,32,32,32]{3,2,1,0:T(8,128)(2,1)} reshape(bf16[1,32,32,1024]{3,2,1,0:T(8,128)(2,1)} %get-tuple-element.55) | data formatting | bytes 4194304 | tf_op jit(solution)/shard_map/reshape;squeeze | solution.py:51
  390.1 7.1 %fusion.180 = f32[32,32]{1,0:T(8,128)S(1)} fusion(bf16[32,32,32,32]{3,2,1,0:T(8,128)(2,1)} %reshape_squeeze.52, f32[32,32]{0,1:T(8,128)S(1)} %bitcast.1056, f32[32,32]{1,0:T(8,128)S(1)} %copy.431, f32[32,32]{1,0:T(8,128)S(1)} %copy.433), kind=kOutput, calls=%fused_computation.180 | convolution fusion | flops 67238912 | bytes 2113536 | tf_op jit(solution)/shard_map/abcd,bcr->adr/dot_general | solution.py:40
  402.3 11.0 %reshape_squeeze.53 = bf16[32,32,32,32]{3,2,1,0:T(8,128)(2,1)} reshape(bf16[1,32,32,1024]{3,2,1,0:T(8,128)(2,1)} %get-tuple-element.64) | data formatting | bytes 4194304 | tf_op jit(solution)/shard_map/reshape;squeeze | solution.py:51
  413.4 7.1 %fusion.178 = f32[32,32]{1,0:T(8,128)S(1)} fusion(bf16[32,32,32,32]{3,2,1,0:T(8,128)(2,1)} %reshape_squeeze.53, f32[32,32]{0,1:T(8,128)S(1)} %bitcast.1054, f32[32,32]{1,0:T(8,128)S(1)} %copy.441, f32[32,32]{1,0:T(8,128)S(1)} %copy.443), kind=kOutput, calls=%fused_computation.178 | convolution fusion | flops 67238912 | bytes 2113536 | tf_op jit(solution)/shard_map/abcd,bcr->adr/dot_general | solution.py:40
  425.6 8.1 %reshape_squeeze.54 = bf16[32,32,32,32]{3,2,1,0:T(8,128)(2,1)} reshape(bf16[1,32,32,1024]{3,2,1,0:T(8,128)(2,1)S(1)} %get-tuple-element.54) | data formatting | bytes 4194304 | tf_op jit(solution)/shard_map/reshape;squeeze | solution.py:51
  433.7 7.1 %fusion.176 = f32[32,32]{1,0:T(8,128)S(1)} fusion(bf16[32,32,32,32]{3,2,1,0:T(8,128)(2,1)} %reshape_squeeze.54, f32[32,32]{0,1:T(8,128)S(1)} %bitcast.1052, f32[32,32]{1,0:T(8,128)S(1)} %copy.451, f32[32,32]{1,0:T(8,128)S(1)} %copy.453), kind=kOutput, calls=%fused_computation.176 | convolution fusion | flops 67238912 | bytes 2113536 | tf_op jit(solution)/shard_map/abcd,bcr->adr/dot_general | solution.py:40
  448.7 5.7 collective-permute-done.1
  454.6 5.0 collective-permute-done.2
  459.6 5.0 collective-permute-done.3
  464.8 6.6 collective-permute-done.4
  471.7 5.8 fusion.155
  477.5 6.3 multiply_reduce_fusion
  484.0 5.8 fusion.157
  489.7 5.9 multiply_reduce_fusion.2
  495.8 5.8 fusion.159
  501.5 5.9 multiply_reduce_fusion.4
  507.6 5.8 fusion.161
  513.3 6.1 multiply_reduce_fusion.6
  519.7 5.8 fusion.163
  525.5 5.9 multiply_reduce_fusion.8
  531.5 5.8 fusion.165
  537.3 5.9 multiply_reduce_fusion.10
  543.3 5.8 fusion.167
  549.1 6.1 multiply_reduce_fusion.12
  555.4 5.8 fusion.169
  561.1 5.9 multiply_reduce_fusion.14
  567.2 5.8 fusion.171
  573.0 5.9 multiply_reduce_fusion.16
  579.1 5.8 fusion.173
  584.8 6.3 multiply_reduce_fusion.18
  591.3 5.8 fusion.175
  597.1 6.1 multiply_reduce_fusion.20
  603.2 7.1 %fusion.154 = f32[32,32]{1,0:T(8,128)S(1)} fusion(bf16[32,32,32,32]{3,2,1,0:T(8,128)(2,1)} %reshape_squeeze.54, f32[32,32]{0,1:T(8,128)S(1)} %copy.522, f32[32,32]{1,0:T(8,128)S(1)} %get-tuple-element.65, f32[32,32]{1,0:T(8,128)S(1)} %get-tuple-element.66), kind=kOutput, calls=%fused_computation.154 | convolution fusion | flops 67238912 | bytes 2113536 | tf_op jit(solution)/shard_map/abcd,bcr->adr/dot_general | solution.py:40
  610.3 7.1 %fusion.156 = f32[32,32]{1,0:T(8,128)S(1)} fusion(bf16[32,32,32,32]{3,2,1,0:T(8,128)(2,1)} %reshape_squeeze.53, f32[32,32]{0,1:T(8,128)S(1)} %copy.516, f32[32,32]{1,0:T(8,128)S(1)} %get-tuple-element.70, f32[32,32]{1,0:T(8,128)S(1)} %get-tuple-element.69), kind=kOutput, calls=%fused_computation.156 | convolution fusion | flops 67238912 | bytes 2113536 | tf_op jit(solution)/shard_map/abcd,bcr->adr/dot_general | solution.py:40
  617.4 3.7 fusion.158
  624.8 7.1 %fusion.162 = f32[32,32]{1,0:T(8,128)S(1)} fusion(bf16[32,32,32,32]{3,2,1,0:T(8,128)(2,1)} %reshape_squeeze.50, f32[32,32]{0,1:T(8,128)S(1)} %copy.498, f32[32,32]{1,0:T(8,128)S(1)} %get-tuple-element.82, f32[32,32]{1,0:T(8,128)S(1)} %get-tuple-element.81), kind=kOutput, calls=%fused_computation.162 | convolution fusion | flops 67238912 | bytes 2113536 | tf_op jit(solution)/shard_map/abcd,bcr->adr/dot_general | solution.py:40
  631.9 3.8 fusion.164
  635.7 3.6 fusion.166
  639.4 3.6 fusion.168
  643.0 3.6 fusion.170
  646.6 3.8 fusion.172
  650.5 3.6 fusion.174
  656.9 5.1 collective-permute-done.6
  662.3 4.8 collective-permute-done.7
  667.1 5.0 collective-permute-done.8
  672.8 6.2 collective-permute-done.9
  (282 shorter events, 84.9 us)
Async XLA Ops:
  173.6 18.4 %copy-start.11 = (f32[32,1,256]{2,1,0:T(1,128)}, f32[32,1,256]{2,1,0:T(1,128)S(1)}, u32[]{:S(2)}) copy-start(f32[32,1,256]{2,1,0:T(1,128)S(1)} %all-gather) | copy-start | bytes 98308
  202.9 7.1 %copy-start = (bf16[32,32,32,32]{3,2,1,0:T(8,128)(2,1)S(1)}, bf16[32,32,32,32]{3,2,1,0:T(8,128)(2,1)}, u32[]{:S(2)}) copy-start(bf16[32,32,32,32]{3,2,1,0:T(8,128)(2,1)} %reshape_squeeze.45) | copy-start | bytes 6291460
  226.2 7.1 %copy-start.1 = (bf16[32,32,32,32]{3,2,1,0:T(8,128)(2,1)S(1)}, bf16[32,32,32,32]{3,2,1,0:T(8,128)(2,1)}, u32[]{:S(2)}) copy-start(bf16[32,32,32,32]{3,2,1,0:T(8,128)(2,1)} %reshape_squeeze.44) | copy-start | bytes 6291460
  249.5 7.1 %copy-start.2 = (bf16[32,32,32,32]{3,2,1,0:T(8,128)(2,1)S(1)}, bf16[32,32,32,32]{3,2,1,0:T(8,128)(2,1)}, u32[]{:S(2)}) copy-start(bf16[32,32,32,32]{3,2,1,0:T(8,128)(2,1)} %reshape_squeeze.46) | copy-start | bytes 6291460
  272.9 7.1 %copy-start.3 = (bf16[32,32,32,32]{3,2,1,0:T(8,128)(2,1)S(1)}, bf16[32,32,32,32]{3,2,1,0:T(8,128)(2,1)}, u32[]{:S(2)}) copy-start(bf16[32,32,32,32]{3,2,1,0:T(8,128)(2,1)} %reshape_squeeze.47) | copy-start | bytes 6291460
  296.5 7.1 %copy-start.4 = (bf16[32,32,32,32]{3,2,1,0:T(8,128)(2,1)S(1)}, bf16[32,32,32,32]{3,2,1,0:T(8,128)(2,1)}, u32[]{:S(2)}) copy-start(bf16[32,32,32,32]{3,2,1,0:T(8,128)(2,1)} %reshape_squeeze.48) | copy-start | bytes 6291460
  319.8 7.1 %copy-start.5 = (bf16[32,32,32,32]{3,2,1,0:T(8,128)(2,1)S(1)}, bf16[32,32,32,32]{3,2,1,0:T(8,128)(2,1)}, u32[]{:S(2)}) copy-start(bf16[32,32,32,32]{3,2,1,0:T(8,128)(2,1)} %reshape_squeeze.49) | copy-start | bytes 6291460
  343.1 7.1 %copy-start.6 = (bf16[32,32,32,32]{3,2,1,0:T(8,128)(2,1)S(1)}, bf16[32,32,32,32]{3,2,1,0:T(8,128)(2,1)}, u32[]{:S(2)}) copy-start(bf16[32,32,32,32]{3,2,1,0:T(8,128)(2,1)} %reshape_squeeze.50) | copy-start | bytes 6291460
  366.5 7.1 %copy-start.7 = (bf16[32,32,32,32]{3,2,1,0:T(8,128)(2,1)S(1)}, bf16[32,32,32,32]{3,2,1,0:T(8,128)(2,1)}, u32[]{:S(2)}) copy-start(bf16[32,32,32,32]{3,2,1,0:T(8,128)(2,1)} %reshape_squeeze.51) | copy-start | bytes 6291460
  390.1 7.1 %copy-start.8 = (bf16[32,32,32,32]{3,2,1,0:T(8,128)(2,1)S(1)}, bf16[32,32,32,32]{3,2,1,0:T(8,128)(2,1)}, u32[]{:S(2)}) copy-start(bf16[32,32,32,32]{3,2,1,0:T(8,128)(2,1)} %reshape_squeeze.52) | copy-start | bytes 6291460
  413.4 7.1 %copy-start.9 = (bf16[32,32,32,32]{3,2,1,0:T(8,128)(2,1)S(1)}, bf16[32,32,32,32]{3,2,1,0:T(8,128)(2,1)}, u32[]{:S(2)}) copy-start(bf16[32,32,32,32]{3,2,1,0:T(8,128)(2,1)} %reshape_squeeze.53) | copy-start | bytes 6291460
  433.7 7.1 %copy-start.10 = (bf16[32,32,32,32]{3,2,1,0:T(8,128)(2,1)S(1)}, bf16[32,32,32,32]{3,2,1,0:T(8,128)(2,1)}, u32[]{:S(2)}) copy-start(bf16[32,32,32,32]{3,2,1,0:T(8,128)(2,1)} %reshape_squeeze.54) | copy-start | bytes 6291460
  443.2 21.5 %copy-start.12 = (f32[32,1,256]{2,1,0:T(1,128)S(1)}, f32[32,1,256]{2,1,0:T(1,128)}, u32[]{:S(2)}) copy-start(f32[32,1,256]{2,1,0:T(1,128)} %copy-done.11) | copy-start | bytes 98308
  443.2 28.2 %copy-start.13 = (f32[32]{0:T(128)S(1)}, f32[32]{0:T(128)}, u32[]{:S(2)}) copy-start(f32[32]{0:T(128)} %param.7) | copy-start | bytes 388
  447.2 1.4 collective-permute-start
  448.7 5.8 collective-permute-start.1
  454.5 5.0 collective-permute-start.2
  459.6 5.0 collective-permute-start.3
  464.6 6.8 collective-permute-start.4
  597.1 20.2 %slice-start.14 = ((s8[8388608]{0:T(1024)(128)(4,1)}), s8[4194304]{0:T(1024)(128)(4,1)S(1)}, s32[]{:S(2)}) async-start(s8[8388608]{0:T(1024)(128)(4,1)} %bitcast.1049), calls=%async_computation.14 | async-start | bytes 8388608
  603.2 14.2 %slice-start.15 = ((s8[8388608]{0:T(1024)(128)(4,1)}), s8[4194304]{0:T(1024)(128)(4,1)S(1)}, s32[]{:S(2)}) async-start(s8[8388608]{0:T(1024)(128)(4,1)} %bitcast.1049), calls=%async_computation.15 | async-start | bytes 8388608
  603.2 18.0 %slice-start.12 = ((s8[8388608]{0:T(1024)(128)(4,1)}), s8[4194304]{0:T(1024)(128)(4,1)S(1)}, s32[]{:S(2)}) async-start(s8[8388608]{0:T(1024)(128)(4,1)} %bitcast.1047), calls=%async_computation.12 | async-start | bytes 8388608
  610.3 10.9 %slice-start.13 = ((s8[8388608]{0:T(1024)(128)(4,1)}), s8[4194304]{0:T(1024)(128)(4,1)S(1)}, s32[]{:S(2)}) async-start(s8[8388608]{0:T(1024)(128)(4,1)} %bitcast.1047), calls=%async_computation.13 | async-start | bytes 8388608
  617.4 14.5 %slice-start.10 = ((s8[8388608]{0:T(1024)(128)(4,1)}), s8[4194304]{0:T(1024)(128)(4,1)S(1)}, s32[]{:S(2)}) async-start(s8[8388608]{0:T(1024)(128)(4,1)} %bitcast.1045), calls=%async_computation.10 | async-start | bytes 8388608
  621.2 10.7 %slice-start.11 = ((s8[8388608]{0:T(1024)(128)(4,1)}), s8[4194304]{0:T(1024)(128)(4,1)S(1)}, s32[]{:S(2)}) async-start(s8[8388608]{0:T(1024)(128)(4,1)} %bitcast.1045), calls=%async_computation.11 | async-start | bytes 8388608
  621.2 14.5 %slice-start.8 = ((s8[8388608]{0:T(1024)(128)(4,1)}), s8[4194304]{0:T(1024)(128)(4,1)S(1)}, s32[]{:S(2)}) async-start(s8[8388608]{0:T(1024)(128)(4,1)} %bitcast.1043), calls=%async_computation.8 | async-start | bytes 8388608
  624.8 10.9 %slice-start.9 = ((s8[8388608]{0:T(1024)(128)(4,1)}), s8[4194304]{0:T(1024)(128)(4,1)S(1)}, s32[]{:S(2)}) async-start(s8[8388608]{0:T(1024)(128)(4,1)} %bitcast.1043), calls=%async_computation.9 | async-start | bytes 8388608
  624.8 14.5 %slice-start.6 = ((s8[8388608]{0:T(1024)(128)(4,1)}), s8[4194304]{0:T(1024)(128)(4,1)S(1)}, s32[]{:S(2)}) async-start(s8[8388608]{0:T(1024)(128)(4,1)} %bitcast.1041), calls=%async_computation.6 | async-start | bytes 8388608
  631.9 7.4 %slice-start.7 = ((s8[8388608]{0:T(1024)(128)(4,1)}), s8[4194304]{0:T(1024)(128)(4,1)S(1)}, s32[]{:S(2)}) async-start(s8[8388608]{0:T(1024)(128)(4,1)} %bitcast.1041), calls=%async_computation.7 | async-start | bytes 8388608
  631.9 11.1 %slice-start.4 = ((s8[8388608]{0:T(1024)(128)(4,1)}), s8[4194304]{0:T(1024)(128)(4,1)S(1)}, s32[]{:S(2)}) async-start(s8[8388608]{0:T(1024)(128)(4,1)} %bitcast.1039), calls=%async_computation.4 | async-start | bytes 8388608
  635.7 7.2 %slice-start.5 = ((s8[8388608]{0:T(1024)(128)(4,1)}), s8[4194304]{0:T(1024)(128)(4,1)S(1)}, s32[]{:S(2)}) async-start(s8[8388608]{0:T(1024)(128)(4,1)} %bitcast.1039), calls=%async_computation.5 | async-start | bytes 8388608
  639.3 7.2 %slice-start = ((s8[8388608]{0:T(1024)(128)(4,1)}), s8[4194304]{0:T(1024)(128)(4,1)S(1)}, s32[]{:S(2)}) async-start(s8[8388608]{0:T(1024)(128)(4,1)} %bitcast.1035), calls=%async_computation | async-start | bytes 8388608
  639.3 11.1 %slice-start.2 = ((s8[8388608]{0:T(1024)(128)(4,1)}), s8[4194304]{0:T(1024)(128)(4,1)S(1)}, s32[]{:S(2)}) async-start(s8[8388608]{0:T(1024)(128)(4,1)} %bitcast.1037), calls=%async_computation.2 | async-start | bytes 8388608
  643.0 3.6 slice-start.1
  643.0 7.5 %slice-start.3 = ((s8[8388608]{0:T(1024)(128)(4,1)}), s8[4194304]{0:T(1024)(128)(4,1)S(1)}, s32[]{:S(2)}) async-start(s8[8388608]{0:T(1024)(128)(4,1)} %bitcast.1037), calls=%async_computation.3 | async-start | bytes 8388608
  654.9 1.4 collective-permute-start.5
  656.4 5.6 collective-permute-start.6
  662.0 5.0 collective-permute-start.7
  667.0 5.0 collective-permute-start.8
  672.1 6.8 collective-permute-start.9
